TPU v7x, 32 devices: a whole 2x2x4 slice. The times are simulated.
32 devices in a mesh: row: 4 (over x, core), col: 8 (over z, y).
Axes of the slice: x: 2, y: 2, z: 4, core: 2. Of those that a mesh axis runs over, the one named last changes fastest.
Arguments:
- tiles: bfloat16 [4, 8, 128, 128, 128], P('row', 'col')
- tile_row: int32 [4, 8, 128], P('row', 'col'), may hold values from 0 to 15, as said below
- tile_col: int32 [4, 8, 128], P('row', 'col'), may hold values from 0 to 15
- tile_count: int32 [4, 8], P('row', 'col'), may hold values from 1 to 128, as said below
- sinogram: float32 [4, 2048, 128], P('row', 'col')
Outputs:
- volume: float32 [8, 2048, 128], P('col', 'row')
- residual: float32 [4, 2048, 128], P('row', 'col')
Inputs may be any that keep to these rules, and one draw needn't show every extreme that they name: Within one block the pairs (tile_row, tile_col) of all 128 slots are distinct. Slots 0 to tile_count - 1 of a block are live, the rest are ignored; some block has all 128 slots live in every draw.
All inputs are finite; a program needn't handle non-finite values.
Results may differ from a plain program's by a relative error of at most 0.015.
Values may be sent and summed in bfloat16 or wider, within the bound.
A program may use at most 64 MiB of HBM per device.

v0:
```python
import jax
import jax.numpy as jnp
from jax import lax
from jax.sharding import PartitionSpec as P

RT = 16
VT = 16
ITERS = 4


def frame_squares(values):
    return jnp.sum(values * values, axis=(0, 1))


def forward_local(blocks, rows_index, cols_index, count, voxel_block):
    tile = blocks.shape[1]
    frames = voxel_block.shape[1]
    voxel_tiles = voxel_block.reshape(voxel_block.shape[0] // tile, tile, frames)
    picked = jnp.take(voxel_tiles, cols_index, axis=0)
    products = jnp.einsum("tij,tjk->tik", blocks, picked, preferred_element_type=jnp.float32)
    live = jnp.arange(blocks.shape[0], dtype=jnp.int32) < count
    select = (
        (rows_index[None, :] == jnp.arange(RT, dtype=jnp.int32)[:, None]) & live[None, :]
    ).astype(jnp.float32)
    summed = jnp.einsum("ut,tik->uik", select, products, precision=lax.Precision.HIGHEST)
    return summed.reshape(RT * tile, frames)


def backward_local(blocks, rows_index, cols_index, count, ray_block):
    tile = blocks.shape[1]
    frames = ray_block.shape[1]
    ray_tiles = ray_block.reshape(ray_block.shape[0] // tile, tile, frames)
    picked = jnp.take(ray_tiles, rows_index, axis=0)
    products = jnp.einsum("tji,tjk->tik", blocks, picked, preferred_element_type=jnp.float32)
    live = jnp.arange(blocks.shape[0], dtype=jnp.int32) < count
    select = (
        (cols_index[None, :] == jnp.arange(VT, dtype=jnp.int32)[:, None]) & live[None, :]
    ).astype(jnp.float32)
    summed = jnp.einsum("ut,tik->uik", select, products, precision=lax.Precision.HIGHEST)
    return summed.reshape(VT * tile, frames)


def local(tiles, tile_row, tile_col, tile_count, sinogram):
    blocks = tiles[0, 0]
    rows_index = tile_row[0, 0]
    cols_index = tile_col[0, 0]
    count = tile_count[0, 0]
    tile = blocks.shape[1]
    frames = sinogram.shape[2]
    voxel_piece = VT * tile // lax.axis_size("row")
    ray_piece = RT * tile // lax.axis_size("col")

    def ray_block_of(state):
        return state[0].astype(jnp.bfloat16)

    def voxel_total(term):
        return lax.psum(term, "row")

    residual = lax.all_gather(sinogram, "col", axis=1, tiled=True)
    volume = jnp.zeros((1, VT * tile, frames), jnp.float32)

    def backward(state):
        return voxel_total(
            backward_local(blocks, rows_index, cols_index, count, ray_block_of(state))[None]
        )

    search = backward(residual)
    gamma = lax.psum(frame_squares(search), "col")
    direction = search
    for step in range(ITERS):
        image = lax.psum(
            forward_local(blocks, rows_index, cols_index, count, direction[0].astype(jnp.bfloat16))[
                None
            ],
            "col",
        )
        alpha = gamma / lax.psum(frame_squares(image), "row")
        volume = volume + alpha * direction
        residual = residual - alpha * image
        if step + 1 < ITERS:
            search = backward(residual)
            fresh = lax.psum(frame_squares(search), "col")
            direction = search + fresh / gamma * direction
            gamma = fresh
    return (
        lax.dynamic_slice_in_dim(volume, lax.axis_index("row") * voxel_piece, voxel_piece, 1),
        lax.dynamic_slice_in_dim(residual, lax.axis_index("col") * ray_piece, ray_piece, 1),
    )


def solution(mesh):
    return jax.shard_map(
        local,
        mesh=mesh,
        in_specs=(
            P("row", "col", None, None, None),
            P("row", "col", None),
            P("row", "col", None),
            P("row", "col"),
            P("row", "col", None),
        ),
        out_specs=(P("col", "row", None), P("row", "col", None)),
        check_vma=False,
    )
```

profile of v0, /device:TPU:0, one launch (start us, length us, event | category | flops | bytes accessed | tf_op | source)
XLA Modules:
  0.0 851.0 jit_solution(9143394102961914901)
XLA Ops:
  9.9 43.2 %all-gather.2.cloned.1.call-done = f32[1,2048,128]{2,1,0:T(8,128)} async-done(((f32[1,256,128]{2,1,0:T(8,128)}), f32[1,2048,128]{2,1,0:T(8,128)}) %all-gather.2.cloned.1.call-update) | async-done | bytes 1048592 | tf_op jit(solution)/shard_map/all_gather | solution.py:59
  65.8 9.3 %copy.15 = f32[128,128,128]{1,0,2:T(8,128)} copy(f32[128,128,128]{2,1,0:T(8,128)} %fusion.30) | data formatting | bytes 16777216 | tf_op jit(solution)/shard_map/tji,tjk->tik/dot_general | solution.py:34
  81.7 35.1 %all-reduce.9.cloned.1.call-done = f32[1,2048,128]{2,1,0:T(8,128)} async-done(((f32[1,2048,128]{2,1,0:T(8,128)}), f32[1,2048,128]{2,1,0:T(8,128)}) %all-reduce.9.cloned.1.call-update) | async-done | bytes 1048592 | tf_op jit(solution)/shard_map/psum | solution.py:57
  121.8 9.9 %fusion.28 = f32[128,128,128]{2,1,0:T(8,128)} fusion(bf16[1,1,128,128,128]{4,3,2,1,0:T(8,128)(2,1)} %param.7, bf16[128,128,128]{2,1,0:T(8,128)(2,1)} %gather_fusion.1, pred[128]{0:T(512)(128)(4,1)S(1)} %get-tuple-element.15), kind=kOutput, calls=%fused_computation.36 | convolution fusion | flops 538968064 | bytes 16777344 | tf_op jit(solution)/shard_map/tij,tjk->tik/dot_general | solution.py:20
  131.7 9.3 %copy.16 = f32[128,128,128]{1,0,2:T(8,128)} copy(f32[128,128,128]{2,1,0:T(8,128)} %fusion.28) | data formatting | bytes 16777216 | tf_op jit(solution)/shard_map/tij,tjk->tik/dot_general | solution.py:20
  147.5 21.7 %psum.113 = f32[128]{0:T(128)S(1)} all-reduce(f32[128]{0:T(128)S(1)} %get-tuple-element.13), channel_id=1, replica_groups=mesh['row'=4,'col'=8] {'col'}, use_global_device_ids=true, to_apply=%region_2.4 | all-reduce | flops 128 | bytes 1024 | tf_op jit(solution)/shard_map/psum | solution.py:68
  169.2 57.2 %all-reduce.11.cloned.1.call-done = f32[1,2048,128]{2,1,0:T(8,128)} async-done(((f32[1,2048,128]{2,1,0:T(8,128)}), f32[1,2048,128]{2,1,0:T(8,128)}) %all-reduce.11.cloned.1.call-update) | async-done | bytes 1048592 | tf_op jit(solution)/shard_map/psum | solution.py:71
  247.7 9.3 %copy.17 = f32[128,128,128]{1,0,2:T(8,128)} copy(f32[128,128,128]{2,1,0:T(8,128)} %fusion.26) | data formatting | bytes 16777216 | tf_op jit(solution)/shard_map/tji,tjk->tik/dot_general | solution.py:34
  263.5 35.4 %all-reduce.13.cloned.1.call-done = f32[1,2048,128]{2,1,0:T(8,128)} async-done(((f32[1,2048,128]{2,1,0:T(8,128)}), f32[1,2048,128]{2,1,0:T(8,128)}) %all-reduce.13.cloned.1.call-update) | async-done | bytes 1048592 | tf_op jit(solution)/shard_map/psum | solution.py:57
  300.5 21.4 %psum.117 = f32[128]{0:T(128)S(1)} all-reduce(f32[128]{0:T(128)S(1)} %multiply_reduce_fusion.5), channel_id=1, replica_groups=mesh['row'=4,'col'=8] {'col'}, use_global_device_ids=true, to_apply=%region_8.10 | all-reduce | flops 128 | bytes 1024 | tf_op jit(solution)/shard_map/psum | solution.py:82
  327.3 9.9 %fusion.24 = f32[128,128,128]{2,1,0:T(8,128)} fusion(bf16[1,1,128,128,128]{4,3,2,1,0:T(8,128)(2,1)} %param.7, bf16[128,128,128]{2,1,0:T(8,128)(2,1)} %gather_fusion.3, pred[128]{0:T(512)(128)(4,1)S(1)} %get-tuple-element.15), kind=kOutput, calls=%fused_computation.32 | convolution fusion | flops 538968064 | bytes 16777344 | tf_op jit(solution)/shard_map/tij,tjk->tik/dot_general | solution.py:20
  337.2 9.3 %copy.18 = f32[128,128,128]{1,0,2:T(8,128)} copy(f32[128,128,128]{2,1,0:T(8,128)} %fusion.24) | data formatting | bytes 16777216 | tf_op jit(solution)/shard_map/tij,tjk->tik/dot_general | solution.py:20
  353.0 75.2 %all-reduce.15.cloned.1.call-done = f32[1,2048,128]{2,1,0:T(8,128)} async-done(((f32[1,2048,128]{2,1,0:T(8,128)}), f32[1,2048,128]{2,1,0:T(8,128)}) %all-reduce.15.cloned.1.call-update) | async-done | bytes 1048592 | tf_op jit(solution)/shard_map/psum | solution.py:71
  450.3 9.3 %copy.19 = f32[128,128,128]{1,0,2:T(8,128)} copy(f32[128,128,128]{2,1,0:T(8,128)} %fusion.22) | data formatting | bytes 16777216 | tf_op jit(solution)/shard_map/tji,tjk->tik/dot_general | solution.py:34
  466.2 35.4 %all-reduce.17.cloned.1.call-done = f32[1,2048,128]{2,1,0:T(8,128)} async-done(((f32[1,2048,128]{2,1,0:T(8,128)}), f32[1,2048,128]{2,1,0:T(8,128)}) %all-reduce.17.cloned.1.call-update) | async-done | bytes 1048592 | tf_op jit(solution)/shard_map/psum | solution.py:57
  503.1 21.4 %psum.121 = f32[128]{0:T(128)S(1)} all-reduce(f32[128]{0:T(128)S(1)} %multiply_reduce_fusion.3), channel_id=1, replica_groups=mesh['row'=4,'col'=8] {'col'}, use_global_device_ids=true, to_apply=%region_14.16 | all-reduce | flops 128 | bytes 1024 | tf_op jit(solution)/shard_map/psum | solution.py:82
  528.9 9.9 %fusion.20 = f32[128,128,128]{2,1,0:T(8,128)} fusion(bf16[1,1,128,128,128]{4,3,2,1,0:T(8,128)(2,1)} %param.7, bf16[128,128,128]{2,1,0:T(8,128)(2,1)} %gather_fusion.5, pred[128]{0:T(512)(128)(4,1)S(1)} %get-tuple-element.15), kind=kOutput, calls=%fused_computation.28 | convolution fusion | flops 538968064 | bytes 16777344 | tf_op jit(solution)/shard_map/tij,tjk->tik/dot_general | solution.py:20
  538.8 9.3 %copy.20 = f32[128,128,128]{1,0,2:T(8,128)} copy(f32[128,128,128]{2,1,0:T(8,128)} %fusion.20) | data formatting | bytes 16777216 | tf_op jit(solution)/shard_map/tij,tjk->tik/dot_general | solution.py:20
  554.7 75.1 %all-reduce.19.cloned.1.call-done = f32[1,2048,128]{2,1,0:T(8,128)} async-done(((f32[1,2048,128]{2,1,0:T(8,128)}), f32[1,2048,128]{2,1,0:T(8,128)}) %all-reduce.19.cloned.1.call-update) | async-done | bytes 1048592 | tf_op jit(solution)/shard_map/psum | solution.py:71
  652.2 9.3 %copy.21 = f32[128,128,128]{1,0,2:T(8,128)} copy(f32[128,128,128]{2,1,0:T(8,128)} %fusion.18) | data formatting | bytes 16777216 | tf_op jit(solution)/shard_map/tji,tjk->tik/dot_general | solution.py:34
  668.0 35.4 %all-reduce.21.cloned.1.call-done = f32[1,2048,128]{2,1,0:T(8,128)} async-done(((f32[1,2048,128]{2,1,0:T(8,128)}), f32[1,2048,128]{2,1,0:T(8,128)}) %all-reduce.21.cloned.1.call-update) | async-done | bytes 1048592 | tf_op jit(solution)/shard_map/psum | solution.py:57
  704.9 21.4 %psum.125 = f32[128]{0:T(128)S(1)} all-reduce(f32[128]{0:T(128)S(1)} %multiply_reduce_fusion.1), channel_id=1, replica_groups=mesh['row'=4,'col'=8] {'col'}, use_global_device_ids=true, to_apply=%region_20.22 | all-reduce | flops 128 | bytes 1024 | tf_op jit(solution)/shard_map/psum | solution.py:82
  731.8 9.9 %fusion.16 = f32[128,128,128]{2,1,0:T(8,128)} fusion(bf16[1,1,128,128,128]{4,3,2,1,0:T(8,128)(2,1)} %param.7, bf16[128,128,128]{2,1,0:T(8,128)(2,1)} %gather_fusion.7, pred[128]{0:T(512)(128)(4,1)S(1)} %get-tuple-element.15), kind=kOutput, calls=%fused_computation.24 | convolution fusion | flops 538968064 | bytes 16777344 | tf_op jit(solution)/shard_map/tij,tjk->tik/dot_general | solution.py:20
  757.5 75.3 %all-reduce.23.cloned.1.call-done = f32[1,2048,128]{2,1,0:T(8,128)} async-done(((f32[1,2048,128]{2,1,0:T(8,128)}), f32[1,2048,128]{2,1,0:T(8,128)}) %all-reduce.23.cloned.1.call-update) | async-done | bytes 1048592 | tf_op jit(solution)/shard_map/psum | solution.py:71
  (93 shorter events, 178.4 us)
Async XLA Ops:
  7.2 46.0 %all-gather.2.cloned.1.call-start = ((), (), s32[]{:S(2)}) async-start(), calls=%async_computation | async-start | bytes 1179648 | tf_op jit(solution)/shard_map/all_gather | solution.py:59
  7.9 108.9 %all-reduce.9.cloned.1.call-start = ((), (), s32[]{:S(2)}) async-start(), calls=%async_computation.1 | async-start | bytes 2097152 | tf_op jit(solution)/shard_map/psum | solution.py:57
  65.8 9.3 %copy-start.4 = (s32[1,1,128]{2,1,0:T(1,128)S(1)}, s32[1,1,128]{2,1,0:T(1,128)}, u32[]{:S(2)}) copy-start(s32[1,1,128]{2,1,0:T(1,128)} %param.9) | copy-start | bytes 1540
  81.7 144.8 %all-reduce.11.cloned.1.call-start = ((), (), s32[]{:S(2)}) async-start(), calls=%async_computation.2 | async-start | bytes 2097152 | tf_op jit(solution)/shard_map/psum | solution.py:71
  131.7 9.3 %copy-start.5 = (s32[1,1,128]{2,1,0:T(1,128)S(1)}, s32[1,1,128]{2,1,0:T(1,128)}, u32[]{:S(2)}) copy-start(s32[1,1,128]{2,1,0:T(1,128)} %param.8) | copy-start | bytes 1540
  146.1 88.8 %copy-start = (f32[1,2048,128]{2,1,0:T(8,128)S(1)}, f32[1,2048,128]{2,1,0:T(8,128)}, u32[]{:S(2)}) copy-start(f32[1,2048,128]{2,1,0:T(8,128)} %all-gather.2.cloned.1.call-done) | copy-start | bytes 3145732
  147.5 151.5 %all-reduce.13.cloned.1.call-start = ((), (), s32[]{:S(2)}) async-start(), calls=%async_computation.3 | async-start | bytes 2097152 | tf_op jit(solution)/shard_map/psum | solution.py:57
  262.1 59.7 %copy-start.2 = (f32[1,2048,128]{2,1,0:T(8,128)S(1)}, f32[1,2048,128]{2,1,0:T(8,128)}, u32[]{:S(2)}) copy-start(f32[1,2048,128]{2,1,0:T(8,128)} %all-reduce.9.cloned.1.call-done) | copy-start | bytes 3145732
  263.5 164.8 %all-reduce.15.cloned.1.call-start = ((), (), s32[]{:S(2)}) async-start(), calls=%async_computation.4 | async-start | bytes 2097152 | tf_op jit(solution)/shard_map/psum | solution.py:71
  351.6 84.9 %copy-start.1 = (f32[1,2048,128]{2,1,0:T(8,128)S(1)}, f32[1,2048,128]{2,1,0:T(8,128)}, u32[]{:S(2)}) copy-start(f32[1,2048,128]{2,1,0:T(8,128)} %all-reduce.11.cloned.1.call-done) | copy-start | bytes 3145732
  353.0 148.6 %all-reduce.17.cloned.1.call-start = ((), (), s32[]{:S(2)}) async-start(), calls=%async_computation.5 | async-start | bytes 2097152 | tf_op jit(solution)/shard_map/psum | solution.py:57
  464.8 59.7 %copy-start.3 = (f32[1,2048,128]{2,1,0:T(8,128)S(1)}, f32[1,2048,128]{2,1,0:T(8,128)}, u32[]{:S(2)}) copy-start(f32[1,2048,128]{2,1,0:T(8,128)} %get-tuple-element.12) | copy-start | bytes 3145732
  466.1 163.7 %all-reduce.19.cloned.1.call-start = ((), (), s32[]{:S(2)}) async-start(), calls=%async_computation.6 | async-start | bytes 2097152 | tf_op jit(solution)/shard_map/psum | solution.py:71
  554.6 148.8 %all-reduce.21.cloned.1.call-start = ((), (), s32[]{:S(2)}) async-start(), calls=%async_computation.7 | async-start | bytes 2097152 | tf_op jit(solution)/shard_map/psum | solution.py:57
  668.0 164.8 %all-reduce.23.cloned.1.call-start = ((), (), s32[]{:S(2)}) async-start(), calls=%async_computation.8 | async-start | bytes 2097152 | tf_op jit(solution)/shard_map/psum | solution.py:71
Sparse Core Ops, SparseCore 0:
  10.1 42.9 all-gather.1
  81.8 34.9 all-reduce.8
  147.6 78.7 all-reduce.10
  263.6 35.3 all-reduce.12
  353.1 75.1 all-reduce.14
  466.3 35.3 all-reduce.16
  554.8 75.0 all-reduce.18
  668.1 35.3 all-reduce.20
  757.6 75.1 all-reduce.22
where the time goes:
time: 861 us; the launch traced here: 851 us
  waiting for transfers between devices  468 us (54%)
  matrix products  114 us (13%)
  blocking collectives  113 us (13%)
  local copies, waits for them, and re-layouts  109 us (13%)
  other arithmetic  31.2 us (4%)
  between operations  14.9 us (2%)
    psum x4, waiting for transfers between devices, local(): lax.psum(forward_local(blocks, rows_index, cols_index, count, direction[0...  283 us
    psum x4, waiting for transfers between devices, voxel_total(): return lax.psum(term, 'row')  141 us
    psum x3, blocking collectives, local(): fresh = lax.psum(frame_squares(search), 'col')  64.1 us
    all_gather x1, waiting for transfers between devices, local(): residual = lax.all_gather(sinogram, 'col', axis=1, tiled=True)  43.2 us
    dot_general x4, matrix products, forward_local(): jnp.einsum('tij,tjk->tik', blocks, picked, preferred_element_type=jnp.flo...  39.7 us
    dot_general x4, local copies, waits for them, and re-layouts, backward_local(): jnp.einsum('tji,tjk->tik', blocks, picked, preferred_element_type=jnp.flo...  37.1 us
    dot_general x4, local copies, waits for them, and re-layouts, forward_local(): jnp.einsum('tij,tjk->tik', blocks, picked, preferred_element_type=jnp.flo...  37.1 us
    dot_general x4, matrix products, backward_local(): jnp.einsum('tji,tjk->tik', blocks, picked, preferred_element_type=jnp.flo...  33.5 us
  transfers between devices with their start and end apart: 9, of which 9 were waited for; matrix products, arithmetic and copies ran while one was open for 0% of the time, Pallas kernels for 0%

commit v1 on v0

--- a/solution.py
+++ b/solution.py
@@ -68,11 +68,14 @@
     gamma = lax.psum(frame_squares(search), "col")
     direction = search
     for step in range(ITERS):
-        image = lax.psum(
-            forward_local(blocks, rows_index, cols_index, count, direction[0].astype(jnp.bfloat16))[
-                None
-            ],
-            "col",
+        image = jnp.sum(
+            lax.all_gather(
+                forward_local(
+                    blocks, rows_index, cols_index, count, direction[0].astype(jnp.bfloat16)
+                )[None],
+                "col",
+            ),
+            axis=0,
         )
         alpha = gamma / lax.psum(frame_squares(image), "row")
         volume = volume + alpha * direction

time: 861 us -> 1050 us (1.22)
  waiting for transfers between devices: 468 us -> 650 us
  other arithmetic: 31.2 us -> 43.6 us
    all_gather x0 -> x4, waiting for transfers between devices: none -> 467 us  [local(): lax.all_gather(forward_local(blocks, rows_index, cols_index, count, direc...]
    psum x4 -> x0, waiting for transfers between devices: 283 us -> none  [local(): lax.psum(forward_local(blocks, rows_index, cols_index, count, direction[0...]
    reduce_sum x0 -> x4, other arithmetic: none -> 16.7 us  [local(): jnp.sum(lax.all_gather(forward_local(blocks, rows_index, cols_index, coun...]
where the time goes in v1:
time: 1050 us; the launch traced here: 1040 us
  waiting for transfers between devices  650 us (62%)
  matrix products  114 us (11%)
  blocking collectives  110 us (10%)
  local copies, waits for them, and re-layouts  109 us (10%)
  other arithmetic  43.6 us (4%)
  between operations  14.9 us (1%)
    all_gather x4, waiting for transfers between devices, local(): lax.all_gather(forward_local(blocks, rows_index, cols_index, count, direc...  467 us
    psum x4, waiting for transfers between devices, voxel_total(): return lax.psum(term, 'row')  139 us
    psum x3, blocking collectives, local(): fresh = lax.psum(frame_squares(search), 'col')  64.1 us
    all_gather x1, waiting for transfers between devices, local(): residual = lax.all_gather(sinogram, 'col', axis=1, tiled=True)  43.2 us
    dot_general x4, matrix products, forward_local(): jnp.einsum('tij,tjk->tik', blocks, picked, preferred_element_type=jnp.flo...  39.7 us
    dot_general x4, local copies, waits for them, and re-layouts, forward_local(): jnp.einsum('tij,tjk->tik', blocks, picked, preferred_element_type=jnp.flo...  37.1 us
    dot_general x4, local copies, waits for them, and re-layouts, backward_local(): jnp.einsum('tji,tjk->tik', blocks, picked, preferred_element_type=jnp.flo...  37.1 us
    dot_general x4, matrix products, backward_local(): jnp.einsum('tji,tjk->tik', blocks, picked, preferred_element_type=jnp.flo...  33.5 us
  transfers between devices with their start and end apart: 9, of which 9 were waited for; matrix products, arithmetic and copies ran while one was open for 0% of the time, Pallas kernels for 0%

profile of v1, /device:TPU:0, one launch (start us, length us, event | category | flops | bytes accessed | tf_op | source)
XLA Modules:
  0.0 1043.1 jit_solution(1926015520991223598)
XLA Ops:
  9.9 43.2 %all-gather.6.cloned.1.call-done = f32[1,2048,128]{2,1,0:T(8,128)} async-done(((f32[1,256,128]{2,1,0:T(8,128)}), f32[1,2048,128]{2,1,0:T(8,128)}) %all-gather.6.cloned.1.call-update) | async-done | bytes 1048592 | tf_op jit(solution)/shard_map/all_gather | solution.py:59
  65.8 9.3 copy.32
  81.7 35.1 %all-reduce.5.cloned.1.call-done = f32[1,2048,128]{2,1,0:T(8,128)} async-done(((f32[1,2048,128]{2,1,0:T(8,128)}), f32[1,2048,128]{2,1,0:T(8,128)}) %all-reduce.5.cloned.1.call-update) | async-done | bytes 1048592 | tf_op jit(solution)/shard_map/psum | solution.py:57
  121.7 9.9 fusion.37
  131.6 9.3 copy.35
  147.5 22.0 %psum.85 = f32[128]{0:T(128)S(1)} all-reduce(f32[128]{0:T(128)S(1)} %get-tuple-element.13), channel_id=1, replica_groups=mesh['row'=4,'col'=8] {'col'}, use_global_device_ids=true, to_apply=%region_2.4 | all-reduce | flops 128 | bytes 1024 | tf_op jit(solution)/shard_map/psum | solution.py:68
  169.6 103.2 %all-gather.8.cloned.1.call-done = f32[8,1,2048,128]{3,2,1,0:T(8,128)} async-done(((f32[1,1,2048,128]{3,2,1,0:T(8,128)}), f32[8,1,2048,128]{3,2,1,0:T(8,128)}) %all-gather.8.cloned.1.call-update) | async-done | bytes 8388624 | tf_op jit(solution)/shard_map/all_gather | solution.py:72
  294.8 9.3 copy.38
  310.6 34.6 %all-reduce.7.cloned.1.call-done = f32[1,2048,128]{2,1,0:T(8,128)} async-done(((f32[1,2048,128]{2,1,0:T(8,128)}), f32[1,2048,128]{2,1,0:T(8,128)}) %all-reduce.7.cloned.1.call-update) | async-done | bytes 1048592 | tf_op jit(solution)/shard_map/psum | solution.py:57
  346.7 21.4 %psum.88 = f32[128]{0:T(128)S(1)} all-reduce(f32[128]{0:T(128)S(1)} %multiply_reduce_fusion.5), channel_id=1, replica_groups=mesh['row'=4,'col'=8] {'col'}, use_global_device_ids=true, to_apply=%region_8.10 | all-reduce | flops 128 | bytes 1024 | tf_op jit(solution)/shard_map/psum | solution.py:85
  373.5 9.9 fusion.47
  383.4 9.3 copy.41
  399.2 121.4 %all-gather.10.cloned.1.call-done = f32[8,1,2048,128]{3,2,1,0:T(8,128)} async-done(((f32[1,1,2048,128]{3,2,1,0:T(8,128)}), f32[8,1,2048,128]{3,2,1,0:T(8,128)}) %all-gather.10.cloned.1.call-update) | async-done | bytes 8388624 | tf_op jit(solution)/shard_map/all_gather | solution.py:72
  544.7 9.3 copy.44
  560.5 34.6 %all-reduce.9.cloned.1.call-done = f32[1,2048,128]{2,1,0:T(8,128)} async-done(((f32[1,2048,128]{2,1,0:T(8,128)}), f32[1,2048,128]{2,1,0:T(8,128)}) %all-reduce.9.cloned.1.call-update) | async-done | bytes 1048592 | tf_op jit(solution)/shard_map/psum | solution.py:57
  596.6 21.4 %psum.91 = f32[128]{0:T(128)S(1)} all-reduce(f32[128]{0:T(128)S(1)} %multiply_reduce_fusion.3), channel_id=1, replica_groups=mesh['row'=4,'col'=8] {'col'}, use_global_device_ids=true, to_apply=%region_14.16 | all-reduce | flops 128 | bytes 1024 | tf_op jit(solution)/shard_map/psum | solution.py:85
  623.4 9.9 fusion.57
  633.3 9.3 copy.47
  649.2 121.4 %all-gather.12.cloned.1.call-done = f32[8,1,2048,128]{3,2,1,0:T(8,128)} async-done(((f32[1,1,2048,128]{3,2,1,0:T(8,128)}), f32[8,1,2048,128]{3,2,1,0:T(8,128)}) %all-gather.12.cloned.1.call-update) | async-done | bytes 8388624 | tf_op jit(solution)/shard_map/all_gather | solution.py:72
  810.4 34.6 %all-reduce.11.cloned.1.call-done = f32[1,2048,128]{2,1,0:T(8,128)} async-done(((f32[1,2048,128]{2,1,0:T(8,128)}), f32[1,2048,128]{2,1,0:T(8,128)}) %all-reduce.11.cloned.1.call-update) | async-done | bytes 1048592 | tf_op jit(solution)/shard_map/psum | solution.py:57
  846.6 21.4 %psum.94 = f32[128]{0:T(128)S(1)} all-reduce(f32[128]{0:T(128)S(1)} %multiply_reduce_fusion.1), channel_id=1, replica_groups=mesh['row'=4,'col'=8] {'col'}, use_global_device_ids=true, to_apply=%region_20.22 | all-reduce | flops 128 | bytes 1024 | tf_op jit(solution)/shard_map/psum | solution.py:85
  873.3 9.9 fusion.67
  883.3 9.3 copy.53
  899.1 121.4 %all-gather.14.cloned.1.call-done = f32[8,1,2048,128]{3,2,1,0:T(8,128)} async-done(((f32[1,1,2048,128]{3,2,1,0:T(8,128)}), f32[8,1,2048,128]{3,2,1,0:T(8,128)}) %all-gather.14.cloned.1.call-update) | async-done | bytes 8388624 | tf_op jit(solution)/shard_map/all_gather | solution.py:72
  (97 shorter events, 188.1 us)
Async XLA Ops:
  7.2 46.0 %all-gather.6.cloned.1.call-start = ((), (), s32[]{:S(2)}) async-start(), calls=%async_computation | async-start | bytes 1179648 | tf_op jit(solution)/shard_map/all_gather | solution.py:59
  7.9 108.9 %all-reduce.5.cloned.1.call-start = ((), (), s32[]{:S(2)}) async-start(), calls=%async_computation.1 | async-start | bytes 2097152 | tf_op jit(solution)/shard_map/psum | solution.py:57
  65.8 9.3 copy-start.4
  81.6 191.1 %all-gather.8.cloned.1.call-start = ((), (), s32[]{:S(2)}) async-start(), calls=%async_computation.2 | async-start | bytes 9437184 | tf_op jit(solution)/shard_map/all_gather | solution.py:72
  131.6 9.3 copy-start.5
  147.5 197.7 %all-reduce.7.cloned.1.call-start = ((), (), s32[]{:S(2)}) async-start(), calls=%async_computation.3 | async-start | bytes 2097152 | tf_op jit(solution)/shard_map/psum | solution.py:57
  169.6 113.7 %copy-start = (f32[1,2048,128]{2,1,0:T(8,128)S(1)}, f32[1,2048,128]{2,1,0:T(8,128)}, u32[]{:S(2)}) copy-start(f32[1,2048,128]{2,1,0:T(8,128)} %all-gather.6.cloned.1.call-done) | copy-start | bytes 3145732
  309.2 58.9 %copy-start.1 = (f32[1,2048,128]{2,1,0:T(8,128)S(1)}, f32[1,2048,128]{2,1,0:T(8,128)}, u32[]{:S(2)}) copy-start(f32[1,2048,128]{2,1,0:T(8,128)} %all-reduce.5.cloned.1.call-done) | copy-start | bytes 3145732
  310.6 210.1 %all-gather.10.cloned.1.call-start = ((), (), s32[]{:S(2)}) async-start(), calls=%async_computation.4 | async-start | bytes 9437184 | tf_op jit(solution)/shard_map/all_gather | solution.py:72
  399.2 195.9 %all-reduce.9.cloned.1.call-start = ((), (), s32[]{:S(2)}) async-start(), calls=%async_computation.5 | async-start | bytes 2097152 | tf_op jit(solution)/shard_map/psum | solution.py:57
  559.1 58.9 %copy-start.2 = (f32[1,2048,128]{2,1,0:T(8,128)S(1)}, f32[1,2048,128]{2,1,0:T(8,128)}, u32[]{:S(2)}) copy-start(f32[1,2048,128]{2,1,0:T(8,128)} %get-tuple-element.12) | copy-start | bytes 3145732
  560.4 210.1 %all-gather.12.cloned.1.call-start = ((), (), s32[]{:S(2)}) async-start(), calls=%async_computation.6 | async-start | bytes 9437184 | tf_op jit(solution)/shard_map/all_gather | solution.py:72
  649.1 196.0 %all-reduce.11.cloned.1.call-start = ((), (), s32[]{:S(2)}) async-start(), calls=%async_computation.7 | async-start | bytes 2097152 | tf_op jit(solution)/shard_map/psum | solution.py:57
  809.0 58.9 %copy-start.3 = (f32[1,2048,128]{2,1,0:T(8,128)S(1)}, f32[1,2048,128]{2,1,0:T(8,128)}, u32[]{:S(2)}) copy-start(f32[1,2048,128]{2,1,0:T(8,128)} %get-tuple-element.8) | copy-start | bytes 3145732
  810.4 210.1 %all-gather.14.cloned.1.call-start = ((), (), s32[]{:S(2)}) async-start(), calls=%async_computation.8 | async-start | bytes 9437184 | tf_op jit(solution)/shard_map/all_gather | solution.py:72
Sparse Core Ops, SparseCore 0:
  10.1 42.9 all-gather.5
  81.7 34.9 all-reduce.4
  147.6 125.0 all-gather.7
  310.7 34.5 all-reduce.6
  399.3 121.2 all-gather.9
  560.6 34.5 all-reduce.8
  649.2 121.2 all-gather.11
  810.5 34.5 all-reduce.10
  899.2 121.2 all-gather.13
